TPU v7x, 32 devices: a whole 2x2x4 slice. The times are simulated.
32 devices in a mesh: ctx: 8 (over z, x), head: 4 (over y, core).
Axes of the slice: x: 2, y: 2, z: 4, core: 2. Of those that a mesh axis runs over, the one named last changes fastest.
Arguments:
- activations: bfloat16 [8192, 2048], P('ctx', 'head'), may hold values from -6 to 6
- w_query: bfloat16 [2048, 2048], P('ctx', 'head'), may hold values from -0.125 to 0.125
- w_key: bfloat16 [2048, 2048], P('ctx', 'head'), may hold values from -0.125 to 0.125
- w_value: bfloat16 [2048, 2048], P('ctx', 'head'), may hold values from -0.125 to 0.125
- level_table: float32 [16, 64, 14], P('head'), may hold values from 0.2 to 2
- table_rows: int32 [8192], P('ctx'), may hold values from 0 to 63
- out_grad: bfloat16 [8192, 2048], P('ctx', 'head'), may hold values from -0.059814453 to 0.059814453
Outputs:
- attended: bfloat16 [8192, 2048], P('ctx', 'head')
- grad_query: float32 [2048, 2048], P('ctx', 'head')
- grad_key: float32 [2048, 2048], P('ctx', 'head')
- grad_value: float32 [2048, 2048], P('ctx', 'head')
All inputs are finite; a program needn't handle non-finite values.
Results may differ from a plain program's by a relative error of at most 0.0056.
Values may be sent and summed in bfloat16 or wider, within the bound.
A program may use at most 64 MiB of HBM per device.

v0:
```python
import math
import jax
import jax.numpy as jnp
from jax import lax
from jax.sharding import PartitionSpec as P


def from_partner(block, axis, apart):
    count = lax.axis_size(axis)
    route = []
    for low in range(count):
        high = low | 1 << apart
        if high != low and high < count:
            route += [(low, high), (high, low)]
    return lax.ppermute(block, axis, route)


def level_of(distance, bit_total):
    running = jnp.zeros(distance.shape, jnp.int32)
    for bit_num in range(bit_total):
        running = running + (distance >= 1 << bit_num).astype(jnp.int32)
    return running


def on_device(activations, w_query, w_key, w_value, level_table, table_rows, out_grad):
    features = lax.all_gather(activations, "head", axis=1, tiled=True)
    row_count = features.shape[0]
    column_count = w_query.shape[1]
    heads_here = level_table.shape[0]
    table_size = level_table.shape[1]
    level_count = level_table.shape[2]
    head_width = column_count // heads_here
    inner_bits = row_count.bit_length() - 1
    outer_bits = lax.axis_size("ctx").bit_length() - 1
    my_index = lax.axis_index("ctx")
    scale_factor = 1.0 / math.sqrt(head_width * row_count)
    highest = lax.Precision.HIGHEST
    pieces = (
        lax.all_gather(w_query, "ctx", axis=0, tiled=True),
        lax.all_gather(w_key, "ctx", axis=0, tiled=True),
        lax.all_gather(w_value, "ctx", axis=0, tiled=True),
    )
    feature_cols = features
    projected = tuple(
        (
            jnp.dot(feature_cols, weight_piece, preferred_element_type=jnp.float32)
            for weight_piece in pieces
        )
    )
    queries = projected[0].astype(jnp.bfloat16).reshape(row_count, heads_here, head_width)
    key_proj = projected[1].astype(jnp.bfloat16).reshape(row_count, heads_here, head_width)
    value_proj = projected[2].astype(jnp.bfloat16).reshape(row_count, heads_here, head_width)
    grad_heads = out_grad.reshape(row_count, heads_here, head_width)
    onehot = (table_rows[:, None] == jnp.arange(table_size, dtype=jnp.int32)[None, :]).astype(
        jnp.float32
    )
    table_flat = jnp.transpose(level_table, (1, 0, 2)).reshape(table_size, heads_here * level_count)
    lam = jnp.dot(onehot, table_flat, precision=highest).reshape(row_count, heads_here, level_count)
    local_state = jnp.einsum(
        "thd,the->hde", key_proj, value_proj, preferred_element_type=jnp.float32
    )
    block_sum = local_state
    level_list = []
    for bit_num in range(outer_bits):
        sibling = from_partner(block_sum, "ctx", bit_num)
        is_upper = jnp.right_shift(my_index, bit_num) & 1 == 1
        level_list.append(jnp.where(is_upper, sibling, 0.0))
        block_sum = block_sum + sibling
    level_states = jnp.stack(level_list)
    state_narrow = level_states.astype(jnp.bfloat16)
    far_out = jnp.zeros((row_count, heads_here, head_width), jnp.float32)
    query_far = jnp.zeros((row_count, heads_here, head_width), jnp.float32)
    grad_list = []
    for bit_num in range(outer_bits):
        level_weight = lam[:, :, inner_bits + 1 + bit_num]
        far_out = far_out + scale_factor * level_weight[..., None] * jnp.einsum(
            "thd,hde->the", queries, state_narrow[bit_num], preferred_element_type=jnp.float32
        )
        query_far = query_far + scale_factor * level_weight[..., None] * jnp.einsum(
            "the,hde->thd", grad_heads, state_narrow[bit_num], preferred_element_type=jnp.float32
        )
        scaled_query = ((scale_factor * level_weight)[..., None] * queries).astype(jnp.bfloat16)
        grad_list.append(
            jnp.einsum("thd,the->hde", scaled_query, grad_heads, preferred_element_type=jnp.float32)
        )
    pending = jnp.stack(grad_list)
    incoming = jnp.zeros((heads_here, head_width, head_width), jnp.float32)
    for bit_num in range(outer_bits):
        partner = from_partner(pending[bit_num:], "ctx", bit_num)
        is_lower = jnp.right_shift(my_index, bit_num) & 1 == 0
        incoming = incoming + jnp.where(is_lower, partner[0], 0.0)
        pending = jnp.concatenate(
            [pending[: bit_num + 1], pending[bit_num + 1 :] + partner[1:]], axis=0
        )
    back_state = incoming.astype(jnp.bfloat16)
    key_far = jnp.einsum("the,hde->thd", value_proj, back_state, preferred_element_type=jnp.float32)
    value_far = jnp.einsum("thd,hde->the", key_proj, back_state, preferred_element_type=jnp.float32)
    positions = jnp.arange(row_count, dtype=jnp.int32)
    pair_level = level_of(jnp.bitwise_xor(positions[:, None], positions[None, :]), inner_bits + 1)
    causal = positions[:, None] >= positions[None, :]
    near_outs = []
    query_nears = []
    key_nears = []
    value_nears = []
    for head_idx in range(heads_here):
        level_mix = jnp.zeros((row_count, row_count), jnp.float32)
        for level_num in range(inner_bits + 1):
            level_mix = jnp.where(
                pair_level == level_num, lam[:, head_idx, level_num][:, None], level_mix
            )
        level_mix = jnp.where(causal, level_mix * scale_factor, 0.0)
        query_head = queries[:, head_idx]
        key_head = key_proj[:, head_idx]
        value_head = value_proj[:, head_idx]
        grad_head = grad_heads[:, head_idx]
        scores = jnp.dot(query_head, key_head.T, preferred_element_type=jnp.float32)
        attn_probs = (level_mix * scores).astype(jnp.bfloat16)
        near_outs.append(jnp.dot(attn_probs, value_head, preferred_element_type=jnp.float32))
        grad_scores = jnp.dot(grad_head, value_head.T, preferred_element_type=jnp.float32)
        grad_mixed = (level_mix * grad_scores).astype(jnp.bfloat16)
        query_nears.append(jnp.dot(grad_mixed, key_head, preferred_element_type=jnp.float32))
        key_nears.append(jnp.dot(grad_mixed.T, query_head, preferred_element_type=jnp.float32))
        value_nears.append(jnp.dot(attn_probs.T, grad_head, preferred_element_type=jnp.float32))
    attended = (
        (jnp.stack(near_outs, axis=1) + far_out)
        .astype(jnp.bfloat16)
        .reshape(row_count, column_count)
    )
    query_total = (
        (jnp.stack(query_nears, axis=1) + query_far)
        .astype(jnp.bfloat16)
        .reshape(row_count, column_count)
    )
    key_total = (
        (jnp.stack(key_nears, axis=1) + key_far)
        .astype(jnp.bfloat16)
        .reshape(row_count, column_count)
    )
    value_total = (
        (jnp.stack(value_nears, axis=1) + value_far)
        .astype(jnp.bfloat16)
        .reshape(row_count, column_count)
    )
    merged = jnp.concatenate([query_total, key_total, value_total], axis=1)
    feature_cols = features
    grad_all = lax.psum_scatter(
        jnp.dot(feature_cols.T, merged, preferred_element_type=jnp.float32),
        "ctx",
        scatter_dimension=0,
        tiled=True,
    )
    grad_query = grad_all[:, :column_count]
    grad_key = grad_all[:, column_count : 2 * column_count]
    grad_value = grad_all[:, 2 * column_count :]
    return (attended, grad_query, grad_key, grad_value)


def solution(mesh):
    return jax.shard_map(
        on_device,
        mesh=mesh,
        in_specs=(
            P("ctx", "head"),
            P("ctx", "head"),
            P("ctx", "head"),
            P("ctx", "head"),
            P("head", None, None),
            P("ctx"),
            P("ctx", "head"),
        ),
        out_specs=(P("ctx", "head"), P("ctx", "head"), P("ctx", "head"), P("ctx", "head")),
        check_vma=False,
    )
```

profile of v0, /device:TPU:0, one launch (start us, length us, event | category | flops | bytes accessed | tf_op | source)
XLA Modules:
  0.0 552.1 jit_solution(5934484398656798456)
XLA Ops:
  14.7 47.3 %all-gather.9.cloned.1.call-done = bf16[2048,512]{1,0:T(8,128)(2,1)} async-done(((bf16[256,512]{1,0:T(8,128)(2,1)}), bf16[2048,512]{1,0:T(8,128)(2,1)}) %all-gather.9.cloned.1.call-update) | async-done | bytes 2097168 | tf_op jit(solution)/shard_map/all_gather | solution.py:40
  61.9 34.6 %all-gather.5.cloned.1.call-done = bf16[1024,2048]{1,0:T(8,128)(2,1)} async-done(((bf16[1024,512]{1,0:T(8,128)(2,1)}), bf16[1024,2048]{1,0:T(8,128)(2,1)}) %all-gather.5.cloned.1.call-update) | async-done | bytes 4194320 | tf_op jit(solution)/shard_map/all_gather | solution.py:26
  96.5 5.2 convolution_convert_fusion.1
  101.8 46.0 %all-gather.11.cloned.1.call-done = bf16[2048,512]{1,0:T(8,128)(2,1)} async-done(((bf16[256,512]{1,0:T(8,128)(2,1)}), bf16[2048,512]{1,0:T(8,128)(2,1)}) %all-gather.11.cloned.1.call-update) | async-done | bytes 2097168 | tf_op jit(solution)/shard_map/all_gather | solution.py:41
  147.8 5.2 convolution_convert_fusion
  153.0 9.0 %fusion = bf16[1024,1024]{1,0:T(8,128)(2,1)S(1)} fusion(f32[1024]{0:T(1024)S(1)} %bitcast.392, f32[1024]{0:T(1024)S(1)} %bitcast.394, f32[1024]{0:T(1024)S(1)} %bitcast.396, f32[1024]{0:T(1024)S(1)} %bitcast.398, f32[1024]{0:T(1024)S(1)} %bitcast.400, f32[1024]{0:T(1024)S(1)} %bitcast.402, f32[1024]{0:T(1024)S(1)} %bitcast.404, f32[1024]{0:T(1024)S(1)} %bitcast.406, ...), kind=kOutput, calls=%fused_computation.2 | convolution fusion | flops 331350016 | bytes 2666496 | tf_op jit(solution)/shard_map/dot_general | solution.py:119
  163.4 1.6 convolution_bitcast_fusion.9
  166.2 31.2 %all-gather.7.cloned.1.call-done = bf16[2048,512]{1,0:T(8,128)(2,1)} async-done(((bf16[256,512]{1,0:T(8,128)(2,1)}), bf16[2048,512]{1,0:T(8,128)(2,1)}) %all-gather.7.cloned.1.call-update) | async-done | bytes 2097168 | tf_op jit(solution)/shard_map/all_gather | solution.py:39
  197.4 5.4 convolution_convert_fusion.2
  203.3 9.5 %multiply_convert_fusion = bf16[1024,1024]{1,0:T(8,128)(2,1)S(1)} fusion(f32[1024]{0:T(1024)S(1)} %bitcast.393, f32[1024]{0:T(1024)S(1)} %bitcast.395, f32[1024]{0:T(1024)S(1)} %bitcast.397, f32[1024]{0:T(1024)S(1)} %bitcast.399, f32[1024]{0:T(1024)S(1)} %bitcast.401, f32[1024]{0:T(1024)S(1)} %bitcast.403, f32[1024]{0:T(1024)S(1)} %bitcast.405, ...), kind=kOutput, calls=%fused_computation.9 | convolution fusion | flops 331350016 | bytes 2666496 | tf_op jit(solution)/shard_map/dot_general | solution.py:116
  212.8 9.0 %fusion.1 = bf16[1024,1024]{1,0:T(8,128)(2,1)S(1)} fusion(f32[1024]{0:T(1024)S(1)} %bitcast.378, f32[1024]{0:T(1024)S(1)} %bitcast.380, f32[1024]{0:T(1024)S(1)} %bitcast.382, f32[1024]{0:T(1024)S(1)} %bitcast.384, f32[1024]{0:T(1024)S(1)} %bitcast.386, f32[1024]{0:T(1024)S(1)} %bitcast.388, f32[1024]{0:T(1024)S(1)} %bitcast.390, f32[1024]{0:T(1024)S(1)} %bitcast.356, ...), kind=kOutput, calls=%fused_computation.4 | convolution fusion | flops 331350016 | bytes 2666496 | tf_op jit(solution)/shard_map/dot_general | solution.py:119
  223.1 9.0 %multiply_convert_fusion.1 = bf16[1024,1024]{1,0:T(8,128)(2,1)S(1)} fusion(f32[1024]{0:T(1024)S(1)} %bitcast.379, f32[1024]{0:T(1024)S(1)} %bitcast.381, f32[1024]{0:T(1024)S(1)} %bitcast.383, f32[1024]{0:T(1024)S(1)} %bitcast.385, f32[1024]{0:T(1024)S(1)} %bitcast.387, f32[1024]{0:T(1024)S(1)} %bitcast.389, f32[1024]{0:T(1024)S(1)} %bitcast.391, ...), kind=kOutput, calls=%fused_computation.11 | convolution fusion | flops 331350016 | bytes 2666496 | tf_op jit(solution)/shard_map/dot_general | solution.py:116
  232.1 9.0 %fusion.2 = bf16[1024,1024]{1,0:T(8,128)(2,1)S(1)} fusion(f32[1024]{0:T(1024)S(1)} %bitcast.334, f32[1024]{0:T(1024)S(1)} %bitcast.336, f32[1024]{0:T(1024)S(1)} %bitcast.338, f32[1024]{0:T(1024)S(1)} %bitcast.340, f32[1024]{0:T(1024)S(1)} %bitcast.342, f32[1024]{0:T(1024)S(1)} %bitcast.344, f32[1024]{0:T(1024)S(1)} %bitcast.346, f32[1024]{0:T(1024)S(1)} %bitcast.348, ...), kind=kOutput, calls=%fused_computation.6 | convolution fusion | flops 331350016 | bytes 2666496 | tf_op jit(solution)/shard_map/dot_general | solution.py:119
  241.1 9.2 %multiply_convert_fusion.2 = bf16[1024,1024]{1,0:T(8,128)(2,1)S(1)} fusion(f32[1024]{0:T(1024)S(1)} %bitcast.335, f32[1024]{0:T(1024)S(1)} %bitcast.337, f32[1024]{0:T(1024)S(1)} %bitcast.339, f32[1024]{0:T(1024)S(1)} %bitcast.341, f32[1024]{0:T(1024)S(1)} %bitcast.343, f32[1024]{0:T(1024)S(1)} %bitcast.345, f32[1024]{0:T(1024)S(1)} %bitcast.347, ...), kind=kOutput, calls=%fused_computation.13 | convolution fusion | flops 331350016 | bytes 2666496 | tf_op jit(solution)/shard_map/dot_general | solution.py:116
  250.3 9.0 %fusion.3 = bf16[1024,1024]{1,0:T(8,128)(2,1)S(1)} fusion(f32[1024]{0:T(1024)S(1)} %bitcast.328, f32[1024]{0:T(1024)S(1)} %bitcast.330, f32[1024]{0:T(1024)S(1)} %bitcast.332, f32[1024]{0:T(1024)S(1)} %bitcast.368, f32[1024]{0:T(1024)S(1)} %bitcast.370, f32[1024]{0:T(1024)S(1)} %bitcast.372, f32[1024]{0:T(1024)S(1)} %bitcast.374, f32[1024]{0:T(1024)S(1)} %bitcast.376, ...), kind=kOutput, calls=%fused_computation.8 | convolution fusion | flops 331350016 | bytes 2666496 | tf_op jit(solution)/shard_map/dot_general | solution.py:119
  259.3 9.2 %multiply_convert_fusion.3 = bf16[1024,1024]{1,0:T(8,128)(2,1)S(1)} fusion(f32[1024]{0:T(1024)S(1)} %bitcast.329, f32[1024]{0:T(1024)S(1)} %bitcast.331, f32[1024]{0:T(1024)S(1)} %bitcast.333, f32[1024]{0:T(1024)S(1)} %bitcast.369, f32[1024]{0:T(1024)S(1)} %bitcast.371, f32[1024]{0:T(1024)S(1)} %bitcast.373, f32[1024]{0:T(1024)S(1)} %bitcast.375, ...), kind=kOutput, calls=%fused_computation.15 | convolution fusion | flops 331350016 | bytes 2666496 | tf_op jit(solution)/shard_map/dot_general | solution.py:116
  279.4 12.2 %collective-permute-done.3 = f32[3,4,128,128]{3,2,1,0:T(8,128)S(1)} collective-permute-done((f32[3,4,128,128]{3,2,1,0:T(8,128)S(1)}, f32[3,4,128,128]{3,2,1,0:T(8,128)S(1)}, u32[]{:S(2)}, u32[]{:S(2)}) %collective-permute-start.3) | collective-permute-done | bytes 786464 | tf_op jit(solution)/shard_map/ppermute | solution.py:15
  291.7 2.4 collective-permute-start.4
  296.5 10.4 %collective-permute-done.4 = f32[2,4,128,128]{3,2,1,0:T(8,128)S(1)} collective-permute-done((f32[2,4,128,128]{3,2,1,0:T(8,128)S(1)}, f32[2,4,128,128]{3,2,1,0:T(8,128)S(1)}, u32[]{:S(2)}, u32[]{:S(2)}) %collective-permute-start.4) | collective-permute-done | bytes 524320 | tf_op jit(solution)/shard_map/ppermute | solution.py:15
  309.3 11.1 %collective-permute-done.5 = f32[1,4,128,128]{3,2,1,0:T(8,128)S(1)} collective-permute-done((f32[1,4,128,128]{3,2,1,0:T(8,128)S(1)}, f32[1,4,128,128]{3,2,1,0:T(8,128)S(1)}, u32[]{:S(2)}, u32[]{:S(2)}) %collective-permute-start.5) | collective-permute-done | bytes 262176 | tf_op jit(solution)/shard_map/ppermute | solution.py:15
  322.6 12.2 %convolution_bitcast_fusion = f32[2048,1536]{0,1:T(8,128)} fusion(bf16[1024,2048]{1,0:T(8,128)(2,1)S(1)} %copy-done.19, bf16[1024,512]{0,1:T(8,128)(2,1)S(1)} %bitcast.415, bf16[1024,512]{0,1:T(8,128)(2,1)S(1)} %bitcast.414, bf16[1024,512]{0,1:T(8,128)(2,1)S(1)} %bitcast.320), kind=kOutput, calls=%fused_computation | convolution fusion | flops 6451888128 | bytes 19922944 | tf_op jit(solution)/shard_map/dot_general | solution.py:147
  334.8 2.6 convolution_bitcast_fusion.13
  337.4 2.4 convolution_bitcast_fusion.14
  344.8 196.1 %reduce-scatter.2.cloned.1.call-done = f32[256,1536]{0,1:T(8,128)} async-done(((f32[2048,1536]{0,1:T(8,128)}), f32[256,1536]{0,1:T(8,128)}) %reduce-scatter.2.cloned.1.call-update) | async-done | bytes 1572880 | tf_op jit(solution)/shard_map/reduce_scatter | solution.py:146
  (105 shorter events, 38.7 us)
Async XLA Ops:
  7.2 54.8 %all-gather.9.cloned.1.call-start = ((), (), s32[]{:S(2)}) async-start(), calls=%async_computation.3 | async-start | bytes 2359296 | tf_op jit(solution)/shard_map/all_gather | solution.py:40
  7.9 88.6 %all-gather.5.cloned.1.call-start = ((), (), s32[]{:S(2)}) async-start(), calls=%async_computation.1 | async-start | bytes 5242880 | tf_op jit(solution)/shard_map/all_gather | solution.py:26
  8.6 139.1 %all-gather.11.cloned.1.call-start = ((), (), s32[]{:S(2)}) async-start(), calls=%async_computation.4 | async-start | bytes 2359296 | tf_op jit(solution)/shard_map/all_gather | solution.py:41
  9.4 188.0 %all-gather.7.cloned.1.call-start = ((), (), s32[]{:S(2)}) async-start(), calls=%async_computation.2 | async-start | bytes 2359296 | tf_op jit(solution)/shard_map/all_gather | solution.py:39
  10.0 530.9 %reduce-scatter.2.cloned.1.call-start = ((), (), s32[]{:S(2)}) async-start(), calls=%async_computation.5 | async-start | bytes 14155776 | tf_op jit(solution)/shard_map/reduce_scatter | solution.py:146
  101.8 63.3 %copy-start.8 = (bf16[1024,512]{0,1:T(8,128)(2,1)}, bf16[1024,512]{0,1:T(8,128)(2,1)S(1)}, u32[]{:S(2)}) copy-start(bf16[1024,512]{0,1:T(8,128)(2,1)S(1)} %convolution_convert_fusion.1) | copy-start | bytes 3145732
  197.4 5.4 copy-start.7
  197.4 5.8 %copy-start.9 = (bf16[1024,512]{0,1:T(8,128)(2,1)S(1)}, bf16[1024,512]{0,1:T(8,128)(2,1)}, u32[]{:S(2)}) copy-start(bf16[1024,512]{0,1:T(8,128)(2,1)} %copy-done.8) | copy-start | bytes 3145732
  212.8 59.3 %copy-start = (bf16[1024,1024]{1,0:T(8,128)(2,1)}, bf16[1024,1024]{1,0:T(8,128)(2,1)S(1)}, u32[]{:S(2)}) copy-start(bf16[1024,1024]{1,0:T(8,128)(2,1)S(1)} %multiply_convert_fusion) | copy-start | bytes 6291460
  232.1 40.5 %copy-start.1 = (bf16[1024,1024]{1,0:T(8,128)(2,1)}, bf16[1024,1024]{1,0:T(8,128)(2,1)S(1)}, u32[]{:S(2)}) copy-start(bf16[1024,1024]{1,0:T(8,128)(2,1)S(1)} %multiply_convert_fusion.1) | copy-start | bytes 6291460
  250.3 23.2 %copy-start.2 = (bf16[1024,1024]{1,0:T(8,128)(2,1)}, bf16[1024,1024]{1,0:T(8,128)(2,1)S(1)}, u32[]{:S(2)}) copy-start(bf16[1024,1024]{1,0:T(8,128)(2,1)S(1)} %multiply_convert_fusion.2) | copy-start | bytes 6291460
  259.3 9.2 %copy-start.13 = (f32[4,128,128]{2,1,0:T(8,128)S(1)}, f32[4,128,128]{2,1,0:T(8,128)}, u32[]{:S(2)}) copy-start(f32[4,128,128]{2,1,0:T(8,128)} %fusion.60) | copy-start | bytes 786436
  259.3 9.9 %copy-start.15 = (f32[1024,4]{0,1:T(4,128)S(1)}, f32[1024,4]{0,1:T(4,128)}, u32[]{:S(2)}) copy-start(f32[1024,4]{0,1:T(4,128)} %get-tuple-element.66) | copy-start | bytes 49156
  259.3 10.3 %copy-start.17 = (f32[1024,4]{0,1:T(4,128)S(1)}, f32[1024,4]{0,1:T(4,128)}, u32[]{:S(2)}) copy-start(f32[1024,4]{0,1:T(4,128)} %get-tuple-element.67) | copy-start | bytes 49156
  268.5 6.8 %copy-start.4 = (bf16[1024,1024]{1,0:T(8,128)(2,1)}, bf16[1024,1024]{1,0:T(8,128)(2,1)S(1)}, u32[]{:S(2)}) copy-start(bf16[1024,1024]{1,0:T(8,128)(2,1)S(1)} %multiply_convert_fusion.3) | copy-start | bytes 6291460
  268.5 9.2 %collective-permute-start = (f32[4,128,128]{2,1,0:T(8,128)S(1)}, f32[4,128,128]{2,1,0:T(8,128)S(1)}, u32[]{:S(2)}, u32[]{:S(2)}) collective-permute-start(f32[4,128,128]{2,1,0:T(8,128)S(1)} %copy-done.13), channel_id=1, source_target_pairs={{0,4},{4,0},{8,12},{12,8},{16,20},{20,16},{24,28},{28,24},{1,5},{5... | collective-permute-start | bytes 786440 | tf_op jit(solution)/shard_map/ppermute | solution.py:15
  270.6 21.0 %collective-permute-start.3 = (f32[3,4,128,128]{3,2,1,0:T(8,128)S(1)}, f32[3,4,128,128]{3,2,1,0:T(8,128)S(1)}, u32[]{:S(2)}, u32[]{:S(2)}) collective-permute-start(f32[3,4,128,128]{3,2,1,0:T(8,128)S(1)} %pad_maximum_fusion), channel_id=1, source_target_pairs={{0,4},{4,0},{8,12},{12,8},{16,20},{20,16},{24,28},{28,24},{1,5},{5... | collective-permute-start | bytes 2359304 | tf_op jit(solution)/shard_map/ppermute | solution.py:15
  277.8 16.7 %collective-permute-start.1 = (f32[4,128,128]{2,1,0:T(8,128)S(1)}, f32[4,128,128]{2,1,0:T(8,128)S(1)}, u32[]{:S(2)}, u32[]{:S(2)}) collective-permute-start(f32[4,128,128]{2,1,0:T(8,128)S(1)} %add.946), channel_id=1, source_target_pairs={{0,8},{8,0},{4,12},{12,4},{16,24},{24,16},{20,28},{28,20},{1,9},{9... | collective-permute-start | bytes 786440 | tf_op jit(solution)/shard_map/ppermute | solution.py:15
  291.7 16.7 %copy-start.12 = (f32[1024,1,128]{0,2,1:T(8,128)S(1)}, f32[1024,1,128]{0,2,1:T(8,128)}, u32[]{:S(2)}) copy-start(f32[1024,1,128]{0,2,1:T(8,128)} %convolution_bitcast_fusion.9) | copy-start | bytes 1572868
  291.7 15.2 %collective-permute-start.4 = (f32[2,4,128,128]{3,2,1,0:T(8,128)S(1)}, f32[2,4,128,128]{3,2,1,0:T(8,128)S(1)}, u32[]{:S(2)}, u32[]{:S(2)}) collective-permute-start(f32[2,4,128,128]{3,2,1,0:T(8,128)S(1)} %slice_add_fusion), channel_id=1, source_target_pairs={{0,8},{8,0},{4,12},{12,4},{16,24},{24,16},{20,28},{28,20},{1,9},{9... | collective-permute-start | bytes 1572872 | tf_op jit(solution)/shard_map/ppermute | solution.py:15
  294.5 14.7 %copy-start.10 = (f32[4,128,128]{2,1,0:T(8,128)}, f32[4,128,128]{2,1,0:T(8,128)S(1)}, u32[]{:S(2)}) copy-start(f32[4,128,128]{2,1,0:T(8,128)S(1)} %collective-permute-done.1) | copy-start | bytes 786436
  294.6 13.8 %collective-permute-start.2 = (bf16[4,128,128]{2,1,0:T(8,128)(2,1)S(1)}, bf16[4,128,128]{2,1,0:T(8,128)(2,1)S(1)}, u32[]{:S(2)}, u32[]{:S(2)}) collective-permute-start(bf16[4,128,128]{2,1,0:T(8,128)(2,1)S(1)} %add.948), channel_id=1, source_target_pairs={{0,16},{16,0},{4,20},{20,4},{8,24},{24,8},{12,28},{28,12},{1,17},{... | collective-permute-start | bytes 393224 | tf_op jit(solution)/shard_map/ppermute | solution.py:15
  306.9 13.4 %collective-permute-start.5 = (f32[1,4,128,128]{3,2,1,0:T(8,128)S(1)}, f32[1,4,128,128]{3,2,1,0:T(8,128)S(1)}, u32[]{:S(2)}, u32[]{:S(2)}) collective-permute-start(f32[1,4,128,128]{3,2,1,0:T(8,128)S(1)} %slice_add_fusion.1), channel_id=1, source_target_pairs={{0,16},{16,0},{4,20},{20,4},{8,24},{24,8},{12,28},{28,12},{1,17},{... | collective-permute-start | bytes 786440 | tf_op jit(solution)/shard_map/ppermute | solution.py:15
  334.8 5.9 %copy-start.5 = (bf16[1024,1024]{1,0:T(8,128)(2,1)S(1)}, bf16[1024,1024]{1,0:T(8,128)(2,1)}, u32[]{:S(2)}) copy-start(bf16[1024,1024]{1,0:T(8,128)(2,1)} %copy-done.4) | copy-start | bytes 6291460
  (7 other events, 16.0 us)
Sparse Core Ops, SparseCore 0:
  10.1 51.7 all-gather.8
  63.5 32.9 all-gather.4
  98.7 49.0 all-gather.10
  149.8 47.6 all-gather.6
  334.9 205.8 reduce-scatter.1
where the time goes:
time: 560 us; the launch traced here: 552 us
  waiting for transfers between devices  393 us (70%)
  matrix products  123 us (22%)
  between operations  14.7 us (3%)
  local copies, waits for them, and re-layouts  12.1 us (2%)
  starting transfers between devices  9.27 us (2%)
    reduce_scatter x1, waiting for transfers between devices, on_device(): lax.psum_scatter(jnp.dot(feature_cols.T, merged, preferred_element_type=j...  196 us
    all_gather x1, waiting for transfers between devices, on_device(): lax.all_gather(w_key, 'ctx', axis=0, tiled=True)  47.3 us
    all_gather x1, waiting for transfers between devices, on_device(): lax.all_gather(w_value, 'ctx', axis=0, tiled=True)  46 us
    dot_general x4, matrix products, on_device(): scores = jnp.dot(query_head, key_head.T, preferred_element_type=jnp.float32)  36.9 us
    dot_general x4, matrix products, on_device(): jnp.dot(grad_head, value_head.T, preferred_element_type=jnp.float32)  35.9 us
    ppermute x6, waiting for transfers between devices, from_partner(): return lax.ppermute(block, axis, route)  34.8 us
    all_gather x1, waiting for transfers between devices, on_device(): features = lax.all_gather(activations, 'head', axis=1, tiled=True)  34.6 us
    all_gather x1, waiting for transfers between devices, on_device(): lax.all_gather(w_query, 'ctx', axis=0, tiled=True)  31.2 us
  transfers between devices with their start and end apart: 11, of which 9 were waited for; matrix products, arithmetic and copies ran while one was open for 8% of the time, Pallas kernels for 0%

commit v1 on v0

--- a/solution.py
+++ b/solution.py
@@ -23,7 +23,12 @@
 
 
 def on_device(activations, w_query, w_key, w_value, level_table, table_rows, out_grad):
-    features = lax.all_gather(activations, "head", axis=1, tiled=True)
+    ring = [activations]
+    for hop in range(3):
+        ring.append(lax.ppermute(ring[-1], "head", [(dev, (dev + 1) % 4) for dev in range(4)]))
+    features = jnp.roll(
+        jnp.concatenate(ring[::-1], axis=1), (lax.axis_index("head") + 1) * ring[0].shape[1], axis=1
+    )
     row_count = features.shape[0]
     column_count = w_query.shape[1]
     heads_here = level_table.shape[0]

time: 560 us -> 534 us (0.954)
  waiting for transfers between devices: 393 us -> 354 us
  local copies, waits for them, and re-layouts: 12.1 us -> 22.7 us
    all_gather x1, waiting for transfers between devices: 47.3 us -> 0.01 us  [on_device(): lax.all_gather(w_key, 'ctx', axis=0, tiled=True)]
    ppermute x0 -> x3, waiting for transfers between devices: none -> 37.3 us  [on_device(): lax.ppermute(ring[-1], 'head', [(dev, (dev + 1) % 4) for dev in range(4)])]
    all_gather x1 -> x0, waiting for transfers between devices: 34.6 us -> none  [on_device(): features = lax.all_gather(activations, 'head', axis=1, tiled=True)]
    all_gather x1, waiting for transfers between devices: 31.2 us -> 43.4 us  [on_device(): lax.all_gather(w_query, 'ctx', axis=0, tiled=True)]
    unnamed x47 -> x61, local copies, waits for them, and re-layouts: 9.71 us -> 17 us
    all_gather x1, waiting for transfers between devices: 46 us -> 40 us  [on_device(): lax.all_gather(w_value, 'ctx', axis=0, tiled=True)]
  transfers between devices with their start and end apart: 11 -> 13, of which waited for: 9 -> 10; matrix products, arithmetic and copies ran while one was open for 8% -> 9% of each run, Pallas kernels for 0% -> 0%
where the time goes in v1:
time: 534 us; the launch traced here: 525 us
  waiting for transfers between devices  354 us (66%)
  matrix products  124 us (23%)
  local copies, waits for them, and re-layouts  22.7 us (4%)
  between operations  14.9 us (3%)
  starting transfers between devices  9.69 us (2%)
    reduce_scatter x1, waiting for transfers between devices, on_device(): lax.psum_scatter(jnp.dot(feature_cols.T, merged, preferred_element_type=j...  197 us
    all_gather x1, waiting for transfers between devices, on_device(): lax.all_gather(w_query, 'ctx', axis=0, tiled=True)  43.4 us
    all_gather x1, waiting for transfers between devices, on_device(): lax.all_gather(w_value, 'ctx', axis=0, tiled=True)  40 us
    ppermute x3, waiting for transfers between devices, on_device(): lax.ppermute(ring[-1], 'head', [(dev, (dev + 1) % 4) for dev in range(4)])  37.3 us
    dot_general x4, matrix products, on_device(): scores = jnp.dot(query_head, key_head.T, preferred_element_type=jnp.float32)  36.1 us
    dot_general x4, matrix products, on_device(): jnp.dot(grad_head, value_head.T, preferred_element_type=jnp.float32)  36.1 us
    ppermute x6, waiting for transfers between devices, from_partner(): return lax.ppermute(block, axis, route)  35.1 us
    unnamed x61, local copies, waits for them, and re-layouts  17 us
  transfers between devices with their start and end apart: 13, of which 10 were waited for; matrix products, arithmetic and copies ran while one was open for 9% of the time, Pallas kernels for 0%

profile of v1, /device:TPU:0, one launch (start us, length us, event | category | flops | bytes accessed | tf_op | source)
XLA Modules:
  0.0 525.0 jit_solution(8760333317998196761)
XLA Ops:
  9.2 14.6 %collective-permute-done = bf16[1024,512]{1,0:T(8,128)(2,1)S(1)} collective-permute-done((bf16[1024,512]{1,0:T(8,128)(2,1)}, bf16[1024,512]{1,0:T(8,128)(2,1)S(1)}, u32[]{:S(2)}, u32[]{:S(2)}) %collective-permute-start) | collective-permute-done | bytes 1048608 | tf_op jit(solution)/shard_map/ppermute | solution.py:28
  25.7 12.5 %collective-permute-done.1 = bf16[1024,512]{1,0:T(8,128)(2,1)} collective-permute-done((bf16[1024,512]{1,0:T(8,128)(2,1)S(1)}, bf16[1024,512]{1,0:T(8,128)(2,1)}, u32[]{:S(2)}, u32[]{:S(2)}) %collective-permute-start.1) | collective-permute-done | bytes 1048608 | tf_op jit(solution)/shard_map/ppermute | solution.py:28
  42.5 10.2 %collective-permute-done.2 = bf16[1024,512]{1,0:T(8,128)(2,1)} collective-permute-done((bf16[1024,512]{1,0:T(8,128)(2,1)}, bf16[1024,512]{1,0:T(8,128)(2,1)}, u32[]{:S(2)}, u32[]{:S(2)}) %collective-permute-start.2) | collective-permute-done | bytes 1048608 | tf_op jit(solution)/shard_map/ppermute | solution.py:28
  66.5 5.2 fusion.42
  71.7 40.0 %all-gather.8.cloned.1.call-done = bf16[2048,512]{1,0:T(8,128)(2,1)} async-done(((bf16[256,512]{1,0:T(8,128)(2,1)}), bf16[2048,512]{1,0:T(8,128)(2,1)}) %all-gather.8.cloned.1.call-update) | async-done | bytes 2097168 | tf_op jit(solution)/shard_map/all_gather | solution.py:46
  111.7 5.2 fusion.45
  118.1 43.4 %all-gather.4.cloned.1.call-done = bf16[2048,512]{1,0:T(8,128)(2,1)} async-done(((bf16[256,512]{1,0:T(8,128)(2,1)}), bf16[2048,512]{1,0:T(8,128)(2,1)}) %all-gather.4.cloned.1.call-update) | async-done | bytes 2097168 | tf_op jit(solution)/shard_map/all_gather | solution.py:44
  161.5 5.3 %fusion.39 = bf16[1024,512]{0,1:T(8,128)(2,1)S(1)} fusion(bf16[2048,512]{1,0:T(8,128)(2,1)} %all-gather.4.cloned.1.call-done, bf16[1024,4096]{1,0:T(8,128)(2,1)} %constant_dynamic-update-slice_fusion, s32[]{:T(128)S(6)} %select_n.213), kind=kOutput, calls=%fused_computation.78 | convolution fusion | flops 2148007936 | bytes 7340036 | tf_op jit(solution)/shard_map/dot_general | solution.py:51
  166.9 9.0 %multiply_convert_fusion = bf16[1024,1024]{1,0:T(8,128)(2,1)S(1)} fusion(f32[1024]{0:T(1024)S(1)} %bitcast.378, f32[1024]{0:T(1024)S(1)} %bitcast.380, f32[1024]{0:T(1024)S(1)} %bitcast.382, f32[1024]{0:T(1024)S(1)} %bitcast.384, f32[1024]{0:T(1024)S(1)} %bitcast.386, f32[1024]{0:T(1024)S(1)} %bitcast.388, f32[1024]{0:T(1024)S(1)} %bitcast.390, ...), kind=kOutput, calls=%fused_computation.8 | convolution fusion | flops 331350016 | bytes 2666496 | tf_op jit(solution)/shard_map/dot_general | solution.py:121
  175.9 9.2 %fusion = bf16[1024,1024]{1,0:T(8,128)(2,1)S(1)} fusion(f32[1024]{0:T(1024)S(1)} %bitcast.379, f32[1024]{0:T(1024)S(1)} %bitcast.381, f32[1024]{0:T(1024)S(1)} %bitcast.383, f32[1024]{0:T(1024)S(1)} %bitcast.385, f32[1024]{0:T(1024)S(1)} %bitcast.387, f32[1024]{0:T(1024)S(1)} %bitcast.389, f32[1024]{0:T(1024)S(1)} %bitcast.391, f32[1024]{0:T(1024)S(1)} %bitcast.393, ...), kind=kOutput, calls=%fused_computation.1 | convolution fusion | flops 331350016 | bytes 2666496 | tf_op jit(solution)/shard_map/dot_general | solution.py:124
  185.1 9.0 %multiply_convert_fusion.1 = bf16[1024,1024]{1,0:T(8,128)(2,1)S(1)} fusion(f32[1024]{0:T(1024)S(1)} %bitcast.342, f32[1024]{0:T(1024)S(1)} %bitcast.344, f32[1024]{0:T(1024)S(1)} %bitcast.346, f32[1024]{0:T(1024)S(1)} %bitcast.348, f32[1024]{0:T(1024)S(1)} %bitcast.350, f32[1024]{0:T(1024)S(1)} %bitcast.352, f32[1024]{0:T(1024)S(1)} %bitcast.354, ...), kind=kOutput, calls=%fused_computation.10 | convolution fusion | flops 331350016 | bytes 2666496 | tf_op jit(solution)/shard_map/dot_general | solution.py:121
  194.1 9.0 %fusion.1 = bf16[1024,1024]{1,0:T(8,128)(2,1)S(1)} fusion(f32[1024]{0:T(1024)S(1)} %bitcast.343, f32[1024]{0:T(1024)S(1)} %bitcast.345, f32[1024]{0:T(1024)S(1)} %bitcast.347, f32[1024]{0:T(1024)S(1)} %bitcast.349, f32[1024]{0:T(1024)S(1)} %bitcast.351, f32[1024]{0:T(1024)S(1)} %bitcast.353, f32[1024]{0:T(1024)S(1)} %bitcast.355, f32[1024]{0:T(1024)S(1)} %bitcast.401, ...), kind=kOutput, calls=%fused_computation.3 | convolution fusion | flops 331350016 | bytes 2666496 | tf_op jit(solution)/shard_map/dot_general | solution.py:124
  203.1 9.0 %multiply_convert_fusion.2 = bf16[1024,1024]{1,0:T(8,128)(2,1)S(1)} fusion(f32[1024]{0:T(1024)S(1)} %bitcast.356, f32[1024]{0:T(1024)S(1)} %bitcast.358, f32[1024]{0:T(1024)S(1)} %bitcast.360, f32[1024]{0:T(1024)S(1)} %bitcast.362, f32[1024]{0:T(1024)S(1)} %bitcast.364, f32[1024]{0:T(1024)S(1)} %bitcast.366, f32[1024]{0:T(1024)S(1)} %bitcast.368, ...), kind=kOutput, calls=%fused_computation.12 | convolution fusion | flops 331350016 | bytes 2666496 | tf_op jit(solution)/shard_map/dot_general | solution.py:121
  212.1 9.0 %fusion.2 = bf16[1024,1024]{1,0:T(8,128)(2,1)S(1)} fusion(f32[1024]{0:T(1024)S(1)} %bitcast.357, f32[1024]{0:T(1024)S(1)} %bitcast.359, f32[1024]{0:T(1024)S(1)} %bitcast.361, f32[1024]{0:T(1024)S(1)} %bitcast.363, f32[1024]{0:T(1024)S(1)} %bitcast.365, f32[1024]{0:T(1024)S(1)} %bitcast.367, f32[1024]{0:T(1024)S(1)} %bitcast.369, f32[1024]{0:T(1024)S(1)} %bitcast.371, ...), kind=kOutput, calls=%fused_computation.5 | convolution fusion | flops 331350016 | bytes 2666496 | tf_op jit(solution)/shard_map/dot_general | solution.py:124
  221.1 9.2 %multiply_convert_fusion.3 = bf16[1024,1024]{1,0:T(8,128)(2,1)S(1)} fusion(f32[1024]{0:T(1024)S(1)} %bitcast.336, f32[1024]{0:T(1024)S(1)} %bitcast.338, f32[1024]{0:T(1024)S(1)} %bitcast.340, f32[1024]{0:T(1024)S(1)} %bitcast.322, f32[1024]{0:T(1024)S(1)} %bitcast.324, f32[1024]{0:T(1024)S(1)} %bitcast.326, f32[1024]{0:T(1024)S(1)} %bitcast.328, ...), kind=kOutput, calls=%fused_computation.14 | convolution fusion | flops 331350016 | bytes 2666496 | tf_op jit(solution)/shard_map/dot_general | solution.py:121
  230.3 9.0 %fusion.3 = bf16[1024,1024]{1,0:T(8,128)(2,1)S(1)} fusion(f32[1024]{0:T(1024)S(1)} %bitcast.337, f32[1024]{0:T(1024)S(1)} %bitcast.339, f32[1024]{0:T(1024)S(1)} %bitcast.341, f32[1024]{0:T(1024)S(1)} %bitcast.323, f32[1024]{0:T(1024)S(1)} %bitcast.325, f32[1024]{0:T(1024)S(1)} %bitcast.327, f32[1024]{0:T(1024)S(1)} %bitcast.329, f32[1024]{0:T(1024)S(1)} %bitcast.331, ...), kind=kOutput, calls=%fused_computation.7 | convolution fusion | flops 331350016 | bytes 2666496 | tf_op jit(solution)/shard_map/dot_general | solution.py:124
  252.5 12.7 %collective-permute-done.6 = f32[3,4,128,128]{3,2,1,0:T(8,128)S(1)} collective-permute-done((f32[3,4,128,128]{3,2,1,0:T(8,128)S(1)}, f32[3,4,128,128]{3,2,1,0:T(8,128)S(1)}, u32[]{:S(2)}, u32[]{:S(2)}) %collective-permute-start.6) | collective-permute-done | bytes 786464 | tf_op jit(solution)/shard_map/ppermute | solution.py:15
  269.9 10.7 %collective-permute-done.7 = f32[2,4,128,128]{3,2,1,0:T(8,128)S(1)} collective-permute-done((f32[2,4,128,128]{3,2,1,0:T(8,128)S(1)}, f32[2,4,128,128]{3,2,1,0:T(8,128)S(1)}, u32[]{:S(2)}, u32[]{:S(2)}) %collective-permute-start.7) | collective-permute-done | bytes 524320 | tf_op jit(solution)/shard_map/ppermute | solution.py:15
  282.5 11.2 %collective-permute-done.8 = f32[1,4,128,128]{3,2,1,0:T(8,128)S(1)} collective-permute-done((f32[1,4,128,128]{3,2,1,0:T(8,128)S(1)}, f32[1,4,128,128]{3,2,1,0:T(8,128)S(1)}, u32[]{:S(2)}, u32[]{:S(2)}) %collective-permute-start.8) | collective-permute-done | bytes 262176 | tf_op jit(solution)/shard_map/ppermute | solution.py:15
  294.7 14.2 %fusion.15 = f32[2048,1536]{1,0:T(8,128)} fusion(bf16[1024,512]{0,1:T(8,128)(2,1)S(1)} %bitcast.408, bf16[1024,512]{0,1:T(8,128)(2,1)S(1)} %bitcast.409, bf16[1024,512]{0,1:T(8,128)(2,1)S(1)} %bitcast.314, bf16[1024,4096]{1,0:T(8,128)(2,1)} %constant_dynamic-update-slice_fusion, s32[]{:T(128)S(6)} %select_n.213), kind=kOutput, calls=%fused_computation.30 | convolution fusion | flops 6451888128 | bytes 19922948 | tf_op jit(solution)/shard_map/dot_general | solution.py:152
  309.0 2.6 convolution_bitcast_fusion.12
  311.5 2.4 convolution_bitcast_fusion.13
  318.9 196.6 %reduce-scatter.2.cloned.1.call-done = f32[256,1536]{1,0:T(8,128)} async-done(((f32[2048,1536]{1,0:T(8,128)}), f32[256,1536]{1,0:T(8,128)}) %reduce-scatter.2.cloned.1.call-update) | async-done | bytes 1572880 | tf_op jit(solution)/shard_map/reduce_scatter | solution.py:151
  515.5 2.5 fusion.77
  (123 shorter events, 48.5 us)
Async XLA Ops:
  7.2 59.3 %all-gather.6.cloned.1.call-start = ((), (), s32[]{:S(2)}) async-start(), calls=%async_computation.2 | async-start | bytes 2359296 | tf_op jit(solution)/shard_map/all_gather | solution.py:45
  7.9 103.8 %all-gather.8.cloned.1.call-start = ((), (), s32[]{:S(2)}) async-start(), calls=%async_computation.3 | async-start | bytes 2359296 | tf_op jit(solution)/shard_map/all_gather | solution.py:46
  8.6 152.9 %all-gather.4.cloned.1.call-start = ((), (), s32[]{:S(2)}) async-start(), calls=%async_computation.1 | async-start | bytes 2359296 | tf_op jit(solution)/shard_map/all_gather | solution.py:44
  8.7 15.2 %collective-permute-start = (bf16[1024,512]{1,0:T(8,128)(2,1)}, bf16[1024,512]{1,0:T(8,128)(2,1)S(1)}, u32[]{:S(2)}, u32[]{:S(2)}) collective-permute-start(bf16[1024,512]{1,0:T(8,128)(2,1)} %param.7), channel_id=1, source_target_pairs={{0,1},{1,2},{2,3},{3,0},{4,5},{5,6},{6,7},{7,4},{8,9},{9,10},{10,1... | collective-permute-start | bytes 3145736 | tf_op jit(solution)/shard_map/ppermute | solution.py:28
  23.9 14.3 %collective-permute-start.1 = (bf16[1024,512]{1,0:T(8,128)(2,1)S(1)}, bf16[1024,512]{1,0:T(8,128)(2,1)}, u32[]{:S(2)}, u32[]{:S(2)}) collective-permute-start(bf16[1024,512]{1,0:T(8,128)(2,1)S(1)} %collective-permute-done), channel_id=1, source_target_pairs={{0,1},{1,2},{2,3},{3,0},{4,5},{5,6},{6,7},{7,4},{8,9},{9,10},{10,1... | collective-permute-start | bytes 3145736 | tf_op jit(solution)/shard_map/ppermute | solution.py:28
  23.9 491.6 %reduce-scatter.2.cloned.1.call-start = ((), (), s32[]{:S(2)}) async-start(), calls=%async_computation.4 | async-start | bytes 14155776 | tf_op jit(solution)/shard_map/reduce_scatter | solution.py:151
  38.2 14.5 %collective-permute-start.2 = (bf16[1024,512]{1,0:T(8,128)(2,1)}, bf16[1024,512]{1,0:T(8,128)(2,1)}, u32[]{:S(2)}, u32[]{:S(2)}) collective-permute-start(bf16[1024,512]{1,0:T(8,128)(2,1)} %collective-permute-done.1), channel_id=1, source_target_pairs={{0,1},{1,2},{2,3},{3,0},{4,5},{5,6},{6,7},{7,4},{8,9},{9,10},{10,1... | collective-permute-start | bytes 3145736 | tf_op jit(solution)/shard_map/ppermute | solution.py:28
  38.9 19.7 %copy-start.6 = (bf16[1024,512]{1,0:T(8,128)(2,1)S(1)}, bf16[1024,512]{1,0:T(8,128)(2,1)}, u32[]{:S(2)}) copy-start(bf16[1024,512]{1,0:T(8,128)(2,1)} %param.7) | copy-start | bytes 3145732
  71.7 45.2 %copy-start.7 = (bf16[1024,512]{0,1:T(8,128)(2,1)}, bf16[1024,512]{0,1:T(8,128)(2,1)S(1)}, u32[]{:S(2)}) copy-start(bf16[1024,512]{0,1:T(8,128)(2,1)S(1)} %fusion.42) | copy-start | bytes 3145732
  118.1 48.7 %copy-start.17 = (f32[1024,1,1]{0,2,1:T(1,128)S(1)}, f32[1024,1,1]{0,2,1:T(1,128)}, u32[]{:S(2)}) copy-start(f32[1024,1,1]{0,2,1:T(1,128)} %get-tuple-element.30) | copy-start | bytes 12292
  118.1 48.7 %copy-start.18 = (f32[1024,1,1]{0,2,1:T(1,128)S(1)}, f32[1024,1,1]{0,2,1:T(1,128)}, u32[]{:S(2)}) copy-start(f32[1024,1,1]{0,2,1:T(1,128)} %get-tuple-element.31) | copy-start | bytes 12292
  118.1 48.7 %copy-start.19 = (f32[1024,1,1]{0,2,1:T(1,128)S(1)}, f32[1024,1,1]{0,2,1:T(1,128)}, u32[]{:S(2)}) copy-start(f32[1024,1,1]{0,2,1:T(1,128)} %get-tuple-element.32) | copy-start | bytes 12292
  118.1 48.7 %copy-start.20 = (f32[1024,1,1]{0,2,1:T(1,128)S(1)}, f32[1024,1,1]{0,2,1:T(1,128)}, u32[]{:S(2)}) copy-start(f32[1024,1,1]{0,2,1:T(1,128)} %get-tuple-element.33) | copy-start | bytes 12292
  175.9 66.7 %copy-start = (bf16[1024,1024]{1,0:T(8,128)(2,1)}, bf16[1024,1024]{1,0:T(8,128)(2,1)S(1)}, u32[]{:S(2)}) copy-start(bf16[1024,1024]{1,0:T(8,128)(2,1)S(1)} %multiply_convert_fusion) | copy-start | bytes 6291460
  194.1 48.9 %copy-start.1 = (bf16[1024,1024]{1,0:T(8,128)(2,1)}, bf16[1024,1024]{1,0:T(8,128)(2,1)S(1)}, u32[]{:S(2)}) copy-start(bf16[1024,1024]{1,0:T(8,128)(2,1)S(1)} %multiply_convert_fusion.1) | copy-start | bytes 6291460
  212.1 31.4 %copy-start.2 = (bf16[1024,1024]{1,0:T(8,128)(2,1)}, bf16[1024,1024]{1,0:T(8,128)(2,1)S(1)}, u32[]{:S(2)}) copy-start(bf16[1024,1024]{1,0:T(8,128)(2,1)S(1)} %multiply_convert_fusion.2) | copy-start | bytes 6291460
  230.3 13.6 %copy-start.4 = (bf16[1024,1024]{1,0:T(8,128)(2,1)}, bf16[1024,1024]{1,0:T(8,128)(2,1)S(1)}, u32[]{:S(2)}) copy-start(bf16[1024,1024]{1,0:T(8,128)(2,1)S(1)} %multiply_convert_fusion.3) | copy-start | bytes 6291460
  241.9 8.6 %collective-permute-start.3 = (f32[4,128,128]{2,1,0:T(8,128)S(1)}, f32[4,128,128]{2,1,0:T(8,128)S(1)}, u32[]{:S(2)}, u32[]{:S(2)}) collective-permute-start(f32[4,128,128]{2,1,0:T(8,128)S(1)} %copy-done.11), channel_id=1, source_target_pairs={{0,4},{4,0},{8,12},{12,8},{16,20},{20,16},{24,28},{28,24},{1,5},{5... | collective-permute-start | bytes 786440 | tf_op jit(solution)/shard_map/ppermute | solution.py:15
  245.8 19.4 %collective-permute-start.6 = (f32[3,4,128,128]{3,2,1,0:T(8,128)S(1)}, f32[3,4,128,128]{3,2,1,0:T(8,128)S(1)}, u32[]{:S(2)}, u32[]{:S(2)}) collective-permute-start(f32[3,4,128,128]{3,2,1,0:T(8,128)S(1)} %pad_maximum_fusion), channel_id=1, source_target_pairs={{0,4},{4,0},{8,12},{12,8},{16,20},{20,16},{24,28},{28,24},{1,5},{5... | collective-permute-start | bytes 2359304 | tf_op jit(solution)/shard_map/ppermute | solution.py:15
  250.6 17.3 %collective-permute-start.4 = (f32[4,128,128]{2,1,0:T(8,128)S(1)}, f32[4,128,128]{2,1,0:T(8,128)S(1)}, u32[]{:S(2)}, u32[]{:S(2)}) collective-permute-start(f32[4,128,128]{2,1,0:T(8,128)S(1)} %add.962), channel_id=1, source_target_pairs={{0,8},{8,0},{4,12},{12,4},{16,24},{24,16},{20,28},{28,20},{1,9},{9... | collective-permute-start | bytes 786440 | tf_op jit(solution)/shard_map/ppermute | solution.py:15
  265.3 15.2 %collective-permute-start.7 = (f32[2,4,128,128]{3,2,1,0:T(8,128)S(1)}, f32[2,4,128,128]{3,2,1,0:T(8,128)S(1)}, u32[]{:S(2)}, u32[]{:S(2)}) collective-permute-start(f32[2,4,128,128]{3,2,1,0:T(8,128)S(1)} %slice_add_fusion), channel_id=1, source_target_pairs={{0,8},{8,0},{4,12},{12,4},{16,24},{24,16},{20,28},{28,20},{1,9},{9... | collective-permute-start | bytes 1572872 | tf_op jit(solution)/shard_map/ppermute | solution.py:15
  267.9 14.6 %copy-start.9 = (f32[4,128,128]{2,1,0:T(8,128)}, f32[4,128,128]{2,1,0:T(8,128)S(1)}, u32[]{:S(2)}) copy-start(f32[4,128,128]{2,1,0:T(8,128)S(1)} %collective-permute-done.4) | copy-start | bytes 786436
  268.0 13.8 %collective-permute-start.5 = (bf16[4,128,128]{2,1,0:T(8,128)(2,1)S(1)}, bf16[4,128,128]{2,1,0:T(8,128)(2,1)S(1)}, u32[]{:S(2)}, u32[]{:S(2)}) collective-permute-start(bf16[4,128,128]{2,1,0:T(8,128)(2,1)S(1)} %add.964), channel_id=1, source_target_pairs={{0,16},{16,0},{4,20},{20,4},{8,24},{24,8},{12,28},{28,12},{1,17},{... | collective-permute-start | bytes 393224 | tf_op jit(solution)/shard_map/ppermute | solution.py:15
  280.6 13.2 %collective-permute-start.8 = (f32[1,4,128,128]{3,2,1,0:T(8,128)S(1)}, f32[1,4,128,128]{3,2,1,0:T(8,128)S(1)}, u32[]{:S(2)}, u32[]{:S(2)}) collective-permute-start(f32[1,4,128,128]{3,2,1,0:T(8,128)S(1)} %slice_add_fusion.1), channel_id=1, source_target_pairs={{0,16},{16,0},{4,20},{20,4},{8,24},{24,8},{12,28},{28,12},{1,17},{... | collective-permute-start | bytes 786440 | tf_op jit(solution)/shard_map/ppermute | solution.py:15
  (14 other events, 65.3 us)
Sparse Core Ops, SparseCore 0:
  10.1 51.7 all-gather.5
  64.1 47.6 all-gather.7
  113.8 47.6 all-gather.3
  309.1 206.4 reduce-scatter.1
